TPU v7x, 8 devices: a whole 2x2x1 slice. The times are simulated.
8 devices in a mesh: rep: 2 (over y, z), dp: 4 (over x, core).
Axes of the slice: x: 2, y: 2, z: 1, core: 2. Of those that a mesh axis runs over, the one named last changes fastest.
Arguments:
- x: bfloat16 [8, 2048, 512], P(('rep', 'dp')), parts along dimension 0
- dy: bfloat16 [8, 2048, 512], P(('rep', 'dp')), parts along dimension 0
- w_gate: bfloat16 [2, 512, 4096], P(None, 'dp')
- w_up: bfloat16 [2, 512, 4096], P(None, 'dp')
- w_down: bfloat16 [2, 4096, 512], P(None, 'dp')
Outputs:
- output 1: bfloat16 [8, 2048, 512], P(('rep', 'dp')), parts along dimension 0
- output 2: bfloat16 [4, 512, 4096], P('rep', 'dp'), parts along dimension 0
- output 3: bfloat16 [4, 512, 4096], P('rep', 'dp'), parts along dimension 0
- output 4: bfloat16 [4, 4096, 512], P('rep', 'dp'), parts along dimension 0
There are 2 independent parts. A program takes and returns all parts, laid end to end along the dimension named above; an argument that names none is the same for every part.
All inputs are finite; a program needn't handle non-finite values.
Results may differ from a plain program's by a relative error of at most 0.018.
Values are sent between devices in bfloat16 or wider.
A program may use at most 2 GiB of HBM per device.

v0:
```python
import jax
import jax.numpy as jnp
from jax import lax

NAMES = ("w_gate", "w_up", "w_down")


def matmul(a, w):
    return jnp.dot(a, w, preferred_element_type=jnp.float32).astype(jnp.bfloat16)


def normed(h):
    wide = h.astype(jnp.float32)
    scale = lax.rsqrt(jnp.mean(wide**2, -1, keepdims=True) + 1e-6)
    return (wide * scale).astype(jnp.bfloat16)


def layer(h, w):
    a = normed(h)
    gate = jnp.dot(a, w["w_gate"], preferred_element_type=jnp.float32)
    up = jnp.dot(a, w["w_up"], preferred_element_type=jnp.float32)
    return h + matmul((jax.nn.silu(gate) * up).astype(jnp.bfloat16), w["w_down"])


def stack(weights, h):
    for number in range(weights["w_gate"].shape[0]):
        h = layer(h, {name: w[number] for name, w in weights.items()})
    return h


def solution(mesh):
    groups = mesh.shape["rep"]

    def step(x, dy, *weights):
        shape = x.shape
        x, dy = (t.reshape(groups, -1, *t.shape[1:]) for t in (x, dy))

        def of_a_group(x, dy):
            _, back = jax.vjp(stack, dict(zip(NAMES, weights, strict=True)), x)
            by_weights, by_x = back(dy)
            return (by_x, *(by_weights[name] for name in NAMES))

        by_x, *by_weights = jax.vmap(of_a_group)(x, dy)
        return (by_x.reshape(shape), *(t.reshape(-1, *t.shape[2:]) for t in by_weights))

    return step
```

profile of v0, /device:TPU:0, one launch (start us, length us, event | category | flops | bytes accessed | tf_op | source)
XLA Modules:
  0.0 665.8 jit_solution(3288031904892919689)
XLA Ops:
  7.2 3.2 fusion.141
  10.5 1.5 fusion.140
  12.1 3.2 fusion.139
  17.5 2.4 copy.1
  19.9 0.6 multiply_add_fusion.1
  20.5 3.9 copy
  24.4 20.5 %all-gather.30.cloned.1.call-done = bf16[1,512,4096]{2,1,0:T(8,128)(2,1)} async-done(((bf16[1,128,4096]{2,1,0:T(8,128)(2,1)}), bf16[1,512,4096]{2,1,0:T(8,128)(2,1)}) %all-gather.30.cloned.1.call-update) | async-done | bytes 4194320 | tf_op jit(solution)/vmap(jvp())/squeeze | solution.py:27
  45.0 16.9 %fusion.68 = f32[2048,4096]{1,0:T(8,128)} fusion(bf16[1,512,4096]{2,1,0:T(8,128)(2,1)} %all-gather.30.cloned.1.call-done, bf16[1,2048,512]{2,1,0:T(8,128)(2,1)S(1)} %copy-done.1, f32[2048]{0:T(1024)S(1)} %get-tuple-element.13), kind=kOutput, calls=%fused_computation.87 | convolution fusion | flops 8593080320 | bytes 39854080 | tf_op jit(solution)/vmap(jvp())/dot_general | solution.py:20
  61.9 16.7 %all-gather.32.cloned.1.call-done = bf16[1,512,4096]{2,1,0:T(8,128)(2,1)} async-done(((bf16[1,128,4096]{2,1,0:T(8,128)(2,1)}), bf16[1,512,4096]{2,1,0:T(8,128)(2,1)}) %all-gather.32.cloned.1.call-update) | async-done | bytes 4194320 | tf_op jit(solution)/vmap(jvp())/squeeze | solution.py:27
  78.6 16.8 %fusion.64 = f32[2048,4096]{1,0:T(8,128)} fusion(bf16[1,512,4096]{2,1,0:T(8,128)(2,1)} %all-gather.32.cloned.1.call-done, bf16[1,2048,512]{2,1,0:T(8,128)(2,1)S(1)} %copy-done.1, f32[2048]{0:T(1024)S(1)} %get-tuple-element.13), kind=kOutput, calls=%fused_computation.83 | convolution fusion | flops 8593080320 | bytes 39854080 | tf_op jit(solution)/vmap(jvp())/dot_general | solution.py:21
  95.4 27.7 %fusion.24 = bf16[2048,4096]{1,0:T(8,128)(2,1)} fusion(f32[2048,4096]{1,0:T(8,128)} %fusion.64, f32[2048,4096]{1,0:T(8,128)} %fusion.68), kind=kLoop, calls=%fused_computation.34 | loop fusion | flops 50331648 | bytes 83886080
  123.0 14.7 %fusion.49 = (f32[2048]{0:T(1024)S(1)}, bf16[1,1,2048,512]{2,3,1,0:T(8,128)(2,1)}) fusion(bf16[2048,4096]{1,0:T(8,128)(2,1)} %fusion.24, bf16[1,4096,512]{2,1,0:T(8,128)(2,1)} %all-gather.34.cloned.1.call-done, bf16[1,2048,512]{1,2,0:T(8,128)(2,1)S(1)} %copy-done.2), kind=kOutput, calls=%fused_computation.68 | convolution fusion | flops 8595175424 | bytes 25174016 | tf_op jit(solution)/vmap(jvp())/dot_general | solution.py:9
  137.8 0.6 copy-done.10
  138.4 6.2 all-gather.36.cloned.1.call-done
  144.6 18.1 %fusion.58 = f32[2048,4096]{1,0:T(8,128)} fusion(bf16[1,512,4096]{2,1,0:T(8,128)(2,1)} %all-gather.36.cloned.1.call-done, bf16[1,1,2048,512]{2,3,1,0:T(8,128)(2,1)} %get-tuple-element.15, f32[2048]{0:T(1024)S(1)} %bitcast.324), kind=kOutput, calls=%fused_computation.77 | convolution fusion | flops 8593080320 | bytes 39854080 | tf_op jit(solution)/vmap(jvp())/dot_general | solution.py:20
  162.7 15.4 %all-gather.40.cloned.1.call-done = bf16[1,512,4096]{2,1,0:T(8,128)(2,1)} async-done(((bf16[1,128,4096]{2,1,0:T(8,128)(2,1)}), bf16[1,512,4096]{2,1,0:T(8,128)(2,1)}) %all-gather.40.cloned.1.call-update) | async-done | bytes 4194320 | tf_op jit(solution)/vmap(jvp())/squeeze | solution.py:27
  178.1 17.8 %fusion.52 = f32[2048,4096]{1,0:T(8,128)} fusion(bf16[1,512,4096]{2,1,0:T(8,128)(2,1)} %all-gather.40.cloned.1.call-done, bf16[1,1,2048,512]{2,3,1,0:T(8,128)(2,1)} %get-tuple-element.15, f32[2048]{0:T(1024)S(1)} %bitcast.325), kind=kOutput, calls=%fused_computation.71 | convolution fusion | flops 8593080320 | bytes 39854080 | tf_op jit(solution)/vmap(jvp())/dot_general | solution.py:21
  195.9 26.7 %fusion.32 = f32[1,4096,512]{2,1,0:T(8,128)} fusion(f32[2048,4096]{1,0:T(8,128)} %fusion.52, f32[2048,4096]{1,0:T(8,128)} %fusion.58, bf16[1,2048,512]{2,1,0:T(8,128)(2,1)S(1)} %copy-done.7), kind=kOutput, calls=%fused_computation.47 | convolution fusion | flops 8640266240 | bytes 77594624 | tf_op jit(solution)/vmap(transpose(jvp()))/dot_general | solution.py:9
  222.7 14.4 %convolution_convert_fusion.1 = bf16[2048,4096]{1,0:T(8,128)(2,1)} fusion(bf16[1,4096,512]{2,1,0:T(8,128)(2,1)} %all-gather.38.cloned.1.call-done, bf16[1,2048,512]{2,1,0:T(8,128)(2,1)S(1)} %copy-done.7), kind=kOutput, calls=%fused_computation.42 | convolution fusion | flops 8598323200 | bytes 23068672 | tf_op jit(solution)/vmap(transpose(jvp()))/dot_general | solution.py:9
  237.1 27.1 %fusion.4 = bf16[2048,4096]{1,0:T(8,128)(2,1)S(1)} fusion(f32[2048,4096]{1,0:T(8,128)} %fusion.58, f32[2048,4096]{1,0:T(8,128)} %fusion.52, bf16[2048,4096]{1,0:T(8,128)(2,1)} %convolution_convert_fusion.1), kind=kLoop, calls=%fused_computation.10 | loop fusion | flops 100663296 | bytes 100663296
  264.1 5.7 copy-done
  269.9 9.1 %fusion.76 = bf16[2048,512]{0,1:T(8,128)(2,1)S(1)} fusion(bf16[2048,4096]{1,0:T(8,128)(2,1)S(1)} %fusion.4, bf16[1,512,4096]{2,1,0:T(8,128)(2,1)S(1)} %copy-done.17), kind=kOutput, calls=%fused_computation.91 | convolution fusion | flops 8589934592 | bytes 23068672 | tf_op jit(solution)/vmap(transpose(jvp()))/dot_general | solution.py:20
  279.0 21.0 %fusion.51 = (f32[2048]{0:T(1024)S(1)}, bf16[1,1,2048,512]{2,3,1,0:T(8,128)(2,1)S(1)}) fusion(bf16[1,1,2048,512]{2,3,1,0:T(8,128)(2,1)S(1)} %copy-done.8, bf16[2048,512]{0,1:T(8,128)(2,1)S(1)} %fusion.76, bf16[1,512,4096]{2,1,0:T(8,128)(2,1)} %all-gather.40.cloned.1.call-done, bf16[2048,4096]{1,0:T(8,128)(2,1)} %convolution_convert_fusion.1, ...), kind=kOutput, calls=%fused_computation.70 | convolution fusion | flops 8646555648 | bytes 60825600 | tf_op jit(solution)/vmap(transpose(jvp()))/dot_general | solution.py:21
  300.1 1.4 fusion.119
  301.5 15.3 %convolution_bitcast_fusion = f32[1,4096,512]{2,1,0:T(8,128)} fusion(bf16[2048,4096]{1,0:T(8,128)(2,1)} %fusion.24, bf16[1,1,2048,512]{2,3,1,0:T(8,128)(2,1)S(1)} %fusion.119), kind=kOutput, calls=%fused_computation.50 | convolution fusion | flops 8589934592 | bytes 27262976 | tf_op jit(solution)/vmap(transpose(jvp()))/dot_general | solution.py:9
  316.9 14.8 %convolution_convert_fusion = bf16[2048,4096]{1,0:T(8,128)(2,1)} fusion(bf16[1,4096,512]{2,1,0:T(8,128)(2,1)} %all-gather.34.cloned.1.call-done, bf16[1,1,2048,512]{2,3,1,0:T(8,128)(2,1)S(1)} %fusion.119), kind=kOutput, calls=%fused_computation.41 | convolution fusion | flops 8598323200 | bytes 23068672 | tf_op jit(solution)/vmap(transpose(jvp()))/dot_general | solution.py:9
  331.7 33.1 %fusion.7 = bf16[2048,4096]{1,0:T(8,128)(2,1)} fusion(f32[2048,4096]{1,0:T(8,128)} %fusion.68, f32[2048,4096]{1,0:T(8,128)} %fusion.64, bf16[2048,4096]{1,0:T(8,128)(2,1)} %convolution_convert_fusion), kind=kLoop, calls=%fused_computation.13 | loop fusion | flops 100663296 | bytes 100663296
  364.8 22.5 %fusion.35 = f32[1,512,4096]{2,1,0:T(8,128)} fusion(bf16[2048,4096]{1,0:T(8,128)(2,1)} %convolution_convert_fusion.1, f32[2048,4096]{1,0:T(8,128)} %fusion.58, bf16[1,1,2048,512]{2,3,1,0:T(8,128)(2,1)S(1)} %copy-done.9, f32[2048]{0:T(1024)S(1)} %bitcast.327), kind=kOutput, calls=%fused_computation.48 | convolution fusion | flops 8643411968 | bytes 60825600 | tf_op jit(solution)/vmap(transpose(jvp()))/dot_general | solution.py:21
  387.4 14.1 %fusion.70 = bf16[2048,512]{0,1:T(8,128)(2,1)S(1)} fusion(bf16[2048,4096]{1,0:T(8,128)(2,1)} %fusion.7, bf16[1,512,4096]{2,1,0:T(8,128)(2,1)} %all-gather.30.cloned.1.call-done), kind=kOutput, calls=%fused_computation.89 | convolution fusion | flops 8589934592 | bytes 23068672 | tf_op jit(solution)/vmap(transpose(jvp()))/dot_general | solution.py:20
  401.5 20.9 %fusion.47 = (f32[2048]{0:T(1024)S(1)}, bf16[1,1,2048,512]{2,3,1,0:T(8,128)(2,1)}) fusion(bf16[1,2048,512]{1,2,0:T(8,128)(2,1)S(1)} %copy-done.3, bf16[2048,512]{0,1:T(8,128)(2,1)S(1)} %fusion.70, bf16[1,512,4096]{2,1,0:T(8,128)(2,1)S(1)} %copy-done.16, bf16[2048,4096]{1,0:T(8,128)(2,1)} %convolution_convert_fusion, f32[2048,4096]{1,0:T(8,128)} %fusion.68), kind=kOutput, calls=%fused_computation.66 | convolution fusion | flops 8646555648 | bytes 60825600 | tf_op jit(solution)/vmap(transpose(jvp()))/dot_general | solution.py:21
  422.5 22.6 %fusion.38 = f32[1,512,4096]{2,1,0:T(8,128)} fusion(bf16[2048,4096]{1,0:T(8,128)(2,1)} %convolution_convert_fusion, f32[2048,4096]{1,0:T(8,128)} %fusion.68, bf16[1,2048,512]{1,2,0:T(8,128)(2,1)S(1)} %copy-done.3, f32[2048]{0:T(1024)S(1)} %bitcast.329), kind=kOutput, calls=%fused_computation.49 | convolution fusion | flops 8643411968 | bytes 60825600 | tf_op jit(solution)/vmap(transpose(jvp()))/dot_general | solution.py:21
  445.1 0.6 copy-done.15
  445.7 15.3 %convolution_bitcast_fusion.2 = f32[1,512,4096]{2,1,0:T(8,128)} fusion(bf16[2048,4096]{1,0:T(8,128)(2,1)} %copy-done, bf16[1,1,2048,512]{2,3,1,0:T(8,128)(2,1)} %get-tuple-element.15, f32[2048]{0:T(1024)S(1)} %bitcast.328), kind=kOutput, calls=%fused_computation.52 | convolution fusion | flops 8593080320 | bytes 27271168 | tf_op jit(solution)/vmap(transpose(jvp()))/dot_general | solution.py:20
  461.1 14.4 %convolution_bitcast_fusion.1 = f32[1,512,4096]{2,1,0:T(8,128)} fusion(bf16[2048,4096]{1,0:T(8,128)(2,1)} %fusion.7, bf16[1,2048,512]{1,2,0:T(8,128)(2,1)S(1)} %copy-done.3, f32[2048]{0:T(1024)S(1)} %bitcast.330), kind=kOutput, calls=%fused_computation.51 | convolution fusion | flops 8593080320 | bytes 27271168 | tf_op jit(solution)/vmap(transpose(jvp()))/dot_general | solution.py:20
  475.5 4.9 fusion.118
  480.4 3.9 copy.2
  484.3 1.7 convert_bitcast_fusion.1
  486.1 1.7 convert_bitcast_fusion
  487.8 1.5 add_bitcast_fusion
  489.3 1.7 convert_bitcast_fusion.3
  491.0 29.1 %reduce-scatter.25.cloned.1.call-done = f32[1,128,4096]{2,1,0:T(8,128)} async-done(((f32[1,512,4096]{2,1,0:T(8,128)}), f32[1,128,4096]{2,1,0:T(8,128)}) %reduce-scatter.25.cloned.1.call-update) | async-done | bytes 2097168
  520.1 1.7 convert_bitcast_fusion.2
  521.8 1.5 add_bitcast_fusion.1
  523.3 64.5 %reduce-scatter.19.cloned.1.call-done = f32[1,128,4096]{2,1,0:T(8,128)} async-done(((f32[1,512,4096]{2,1,0:T(8,128)}), f32[1,128,4096]{2,1,0:T(8,128)}) %reduce-scatter.19.cloned.1.call-update) | async-done | bytes 2097168
  587.8 1.7 convert_bitcast_fusion.5
  589.5 65.8 %reduce-scatter.21.cloned.1.call-done = f32[1,128,4096]{2,1,0:T(8,128)} async-done(((f32[1,512,4096]{2,1,0:T(8,128)}), f32[1,128,4096]{2,1,0:T(8,128)}) %reduce-scatter.21.cloned.1.call-update) | async-done | bytes 2097168
  655.3 1.7 convert_bitcast_fusion.4
  657.0 1.5 add_bitcast_fusion.2
  (67 shorter events, 2.9 us)
Async XLA Ops:
  7.2 3.3 copy-start.6
  7.2 37.8 %all-gather.30.cloned.1.call-start = ((), (), s32[]{:S(2)}) async-start(), calls=%async_computation.6 | async-start | bytes 5242880 | tf_op jit(solution)/vmap(jvp())/squeeze | solution.py:27
  10.5 68.1 %all-gather.32.cloned.1.call-start = ((), (), s32[]{:S(2)}) async-start(), calls=%async_computation.7 | async-start | bytes 5242880 | tf_op jit(solution)/vmap(jvp())/squeeze | solution.py:27
  12.0 5.1 copy-start.1
  12.0 111.0 %all-gather.34.cloned.1.call-start = ((), (), s32[]{:S(2)}) async-start(), calls=%async_computation.8 | async-start | bytes 5242880 | tf_op jit(solution)/vmap(jvp())/squeeze | solution.py:27
  15.3 129.3 %all-gather.36.cloned.1.call-start = ((), (), s32[]{:S(2)}) async-start(), calls=%async_computation.9 | async-start | bytes 5242880 | tf_op jit(solution)/vmap(jvp())/squeeze | solution.py:27
  15.8 162.2 %all-gather.40.cloned.1.call-start = ((), (), s32[]{:S(2)}) async-start(), calls=%async_computation.11 | async-start | bytes 5242880 | tf_op jit(solution)/vmap(jvp())/squeeze | solution.py:27
  16.4 206.3 %all-gather.38.cloned.1.call-start = ((), (), s32[]{:S(2)}) async-start(), calls=%async_computation.10 | async-start | bytes 5242880 | tf_op jit(solution)/vmap(jvp())/squeeze | solution.py:27
  17.0 467.3 %reduce-scatter.27.cloned.1.call-start = ((), (), s32[]{:S(2)}) async-start(), calls=%async_computation.16 | async-start | bytes 10485760
  95.4 27.7 %copy-start.2 = (bf16[1,2048,512]{1,2,0:T(8,128)(2,1)S(1)}, bf16[1,2048,512]{1,2,0:T(8,128)(2,1)}, u32[]{:S(2)}) copy-start(bf16[1,2048,512]{1,2,0:T(8,128)(2,1)} %copy.1) | copy-start | bytes 6291460
  137.8 0.6 copy-start.10
  138.4 39.7 %copy-start.13 = (f32[1,1,2048]{2,1,0:T(1,128)}, f32[1,1,2048]{2,1,0:T(1,128)S(1)}, u32[]{:S(2)}) copy-start(f32[1,1,2048]{2,1,0:T(1,128)S(1)} %rsqrt.23) | copy-start | bytes 24580
  162.7 33.2 %copy-start.7 = (bf16[1,2048,512]{2,1,0:T(8,128)(2,1)S(1)}, bf16[1,2048,512]{2,1,0:T(8,128)(2,1)}, u32[]{:S(2)}) copy-start(bf16[1,2048,512]{2,1,0:T(8,128)(2,1)} %param) | copy-start | bytes 6291460
  222.6 263.4 %reduce-scatter.29.cloned.1.call-start = ((), (), s32[]{:S(2)}) async-start(), calls=%async_computation.17 | async-start | bytes 10485760
  237.1 32.8 %copy-start.17 = (bf16[1,512,4096]{2,1,0:T(8,128)(2,1)S(1)}, bf16[1,512,4096]{2,1,0:T(8,128)(2,1)}, u32[]{:S(2)}) copy-start(bf16[1,512,4096]{2,1,0:T(8,128)(2,1)} %all-gather.36.cloned.1.call-done) | copy-start | bytes 12582916
  264.1 5.7 copy-start
  269.9 9.1 %copy-start.8 = (bf16[1,1,2048,512]{2,3,1,0:T(8,128)(2,1)S(1)}, bf16[1,1,2048,512]{2,3,1,0:T(8,128)(2,1)}, u32[]{:S(2)}) copy-start(bf16[1,1,2048,512]{2,3,1,0:T(8,128)(2,1)} %get-tuple-element.15) | copy-start | bytes 6291460
  279.0 21.1 %copy-start.11 = (f32[2048]{0:T(1024)S(1)}, f32[2048]{0:T(1024)}, u32[]{:S(2)}) copy-start(f32[2048]{0:T(1024)} %copy-done.10) | copy-start | bytes 24580
  279.0 21.1 %copy-start.4 = (bf16[1,2048,512]{1,2,0:T(8,128)(2,1)S(1)}, bf16[1,2048,512]{1,2,0:T(8,128)(2,1)}, u32[]{:S(2)}) copy-start(bf16[1,2048,512]{1,2,0:T(8,128)(2,1)} %copy) | copy-start | bytes 6291460
  279.0 21.1 %copy-start.14 = (f32[1,1,2048]{2,1,0:T(1,128)S(1)}, f32[1,1,2048]{2,1,0:T(1,128)}, u32[]{:S(2)}) copy-start(f32[1,1,2048]{2,1,0:T(1,128)} %copy-done.13) | copy-start | bytes 24580
  301.5 15.4 %copy-start.5 = (bf16[1,1,2048,512]{2,3,1,0:T(8,128)(2,1)}, bf16[1,1,2048,512]{2,3,1,0:T(8,128)(2,1)S(1)}, u32[]{:S(2)}) copy-start(bf16[1,1,2048,512]{2,3,1,0:T(8,128)(2,1)S(1)} %fusion.119) | copy-start | bytes 6291460
  316.8 172.4 %reduce-scatter.23.cloned.1.call-start = ((), (), s32[]{:S(2)}) async-start(), calls=%async_computation.14 | async-start | bytes 10485760
  331.7 33.1 %copy-start.9 = (bf16[1,1,2048,512]{2,3,1,0:T(8,128)(2,1)S(1)}, bf16[1,1,2048,512]{2,3,1,0:T(8,128)(2,1)}, u32[]{:S(2)}) copy-start(bf16[1,1,2048,512]{2,3,1,0:T(8,128)(2,1)} %get-tuple-element.15) | copy-start | bytes 6291460
  387.3 14.1 %copy-start.3 = (bf16[1,2048,512]{1,2,0:T(8,128)(2,1)S(1)}, bf16[1,2048,512]{1,2,0:T(8,128)(2,1)}, u32[]{:S(2)}) copy-start(bf16[1,2048,512]{1,2,0:T(8,128)(2,1)} %copy.1) | copy-start | bytes 6291460
  387.4 132.8 %reduce-scatter.25.cloned.1.call-start = ((), (), s32[]{:S(2)}) async-start(), calls=%async_computation.15 | async-start | bytes 10485760
  387.4 14.1 %copy-start.16 = (bf16[1,512,4096]{2,1,0:T(8,128)(2,1)S(1)}, bf16[1,512,4096]{2,1,0:T(8,128)(2,1)}, u32[]{:S(2)}) copy-start(bf16[1,512,4096]{2,1,0:T(8,128)(2,1)} %all-gather.32.cloned.1.call-done) | copy-start | bytes 12582916
  401.5 21.0 %copy-start.12 = (f32[2048]{0:T(1024)S(1)}, f32[2048]{0:T(1024)}, u32[]{:S(2)}) copy-start(f32[2048]{0:T(1024)} %get-tuple-element.12) | copy-start | bytes 24580
  445.0 0.7 copy-start.15
  445.1 142.7 %reduce-scatter.19.cloned.1.call-start = ((), (), s32[]{:S(2)}) async-start(), calls=%async_computation.12 | async-start | bytes 10485760
  461.1 194.3 %reduce-scatter.21.cloned.1.call-start = ((), (), s32[]{:S(2)}) async-start(), calls=%async_computation.13 | async-start | bytes 10485760
Sparse Core Ops, SparseCore 0:
  10.6 34.3 all-gather.29
  47.0 31.4 all-gather.31
  80.1 31.4 all-gather.33
  113.0 31.4 all-gather.35
  146.5 31.4 all-gather.39
  179.4 31.4 all-gather.37
  222.8 65.0 reduce-scatter.26
  317.0 65.0 reduce-scatter.28
  387.5 65.0 reduce-scatter.22
  455.0 65.1 reduce-scatter.24
  522.7 65.0 reduce-scatter.18
  590.2 65.1 reduce-scatter.20
where the time goes:
time: 675 us; the launch traced here: 666 us
  matrix products  295 us (44%)
  waiting for transfers between devices  220 us (33%)
  other arithmetic  110 us (16%)
  local copies, waits for them, and re-layouts  25.1 us (4%)
  between operations  15 us (2%)
    unnamed x18, waiting for transfers between devices  161 us
    dot_general x6, matrix products, layer(): up = jnp.dot(a, w['w_up'], preferred_element_type=jnp.float32)  122 us
    dot_general x6, matrix products, layer(): gate = jnp.dot(a, w['w_gate'], preferred_element_type=jnp.float32)  87.8 us
    unnamed x3, other arithmetic  87.8 us
    dot_general x5, matrix products, matmul(): jnp.dot(a, w, preferred_element_type=jnp.float32).astype(jnp.bfloat16)  86 us
    squeeze x6, waiting for transfers between devices, stack(): h = layer(h, {name: w[number] for name, w in weights.items()})  58.8 us
    unnamed x39, local copies, waits for them, and re-layouts  17.2 us
  transfers between devices with their start and end apart: 12, of which 7 were waited for; matrix products, arithmetic and copies ran while one was open for 63% of the time, Pallas kernels for 0%

commit v1 on v0

v1 whole, which is shorter than its diff:
```python
import jax
import jax.numpy as jnp
from jax import lax
from jax.experimental import pallas as pl
from jax.experimental.pallas import tpu as pltpu
from jax.sharding import PartitionSpec as P

f32, bf16 = jnp.float32, jnp.bfloat16
MESH = pl.DeviceIdType.MESH
TT, D, FF, LAYERS = 2048, 512, 4096, 2
FB = 512
NF = FF // FB
UNITS = LAYERS * NF
SLAB = 128
T = 1024
NT = TT // T
TN = 256


def dot(a, b):
    return lax.dot_general(a, b, (((1,), (0,)), ((), ())), preferred_element_type=f32)


def dot_nt(a, b):
    return lax.dot_general(a, b, (((1,), (1,)), ((), ())), preferred_element_type=f32)


def sigmoid(g):
    return 0.5 * jnp.tanh(0.5 * g) + 0.5


def tile(i, size):
    return pl.ds(pl.multiple_of(i * size, size), size)


def rms(wide):
    return lax.rsqrt(jnp.mean(wide * wide, -1, keepdims=True) + 1e-6)


def kernel(
    x_in, dy_in, wg_in, wu_in, wd_in,
    bx_out, dwg_out, dwu_out, dwd_out, WH, RDH, RXH,
    OWN, W, X, A, AT, DY, DYT, H1, ACC, PB, GB, UB, DWB, KEEP, OACC, SD, SX, RDV, RXV, OUTB,
    s_own, s_ownh, s_p, r_p, s_x, r_x, s_y, r_y, s_f, r_f, s_w, s_sd, r_rd, s_rdv, s_sx, r_rx, s_rxv, s_out, s_act,
):
    r, me = lax.axis_index("rep"), lax.axis_index("dp")
    chip, core = me // 2, me % 2
    partner = {"rep": r, "dp": chip * 2 + 1 - core}
    xnbr = {"rep": r, "dp": (1 - chip) * 2 + core}
    ynbr = {"rep": 1 - r, "dp": me}
    far = (1 - chip) * 2 + core

    def rows(d):
        return pl.ds(pl.multiple_of(d * SLAB, SLAB), SLAB)

    def remote(src, dst, send, recv, dev):
        return pltpu.make_async_remote_copy(src_ref=src, dst_ref=dst, send_sem=send, recv_sem=recv, device_id=dev, device_id_type=MESH)

    def order(j):
        return (1 - j // NF) * NF + 2 * ((j % NF) // 2) + lax.rem(r + j, 2)

    def own_loads(u):
        l, f = u // NF, u % NF
        for m, w in enumerate((wg_in, wu_in)):
            for s in range(4):
                yield pltpu.make_async_copy(
                    w.at[l, :, pl.ds(pl.multiple_of(s * 1024 + f * SLAB, SLAB), SLAB)],
                    OWN.at[u, m, :, pl.ds(s * SLAB, SLAB)], s_own.at[u])
        yield pltpu.make_async_copy(wd_in.at[l, tile(f, SLAB), :], OWN.at[u, 2], s_own.at[u])

    def own_home(u):
        return pltpu.make_async_copy(OWN.at[u], WH.at[u, :, rows(me), :], s_ownh.at[u])

    def own_partner(u):
        return remote(OWN.at[u], WH.at[u, :, rows(me), :], s_p.at[u], r_p.at[u], partner)

    def own_x(k):
        u = 2 * k + r
        return remote(OWN.at[u], WH.at[u, :, rows(me), :], s_x.at[k], r_x.at[k], xnbr)

    def forward_y(k):
        u = 2 * k + r
        here = WH.at[u, :, rows(far), :]
        return remote(here, here, s_y.at[k], r_y.at[k], ynbr)

    def forward_partner(u):
        here = WH.at[u, :, rows(far), :]
        return remote(here, here, s_f.at[u], r_f.at[u], partner)

    def arrived_x(k):
        own_x(k).wait_recv()
        forward_y(k).start()
        forward_partner(2 * k + r).start()

    def arrived_y(k):
        forward_y(k).wait_recv()
        forward_partner(2 * k + 1 - r).start()

    def load_w(u, slot):
        return pltpu.make_async_copy(WH.at[u], W.at[slot], s_w.at[slot])

    def fetch_w(u, slot):
        own_partner(u).wait_recv()
        forward_partner(u).wait_recv()
        load_w(u, slot).start()

    def send_terms(u, slot):
        return remote(SD.at[slot], RDH.at[u], s_sd.at[slot], r_rd.at[u], partner)

    def load_terms(u):
        return pltpu.make_async_copy(RDH.at[u], RDV, s_rdv)

    def send_sum(u, slot):
        return remote(SX.at[slot], RXH.at[u], s_sx.at[slot], r_rx.at[u], xnbr)

    def load_sum(u):
        return pltpu.make_async_copy(RXH.at[u], RXV, s_rxv)

    def store_outs(u, slot):
        l, f = u // NF, u % NF
        for m, w in enumerate((dwg_out, dwu_out)):
            for s in range(4):
                yield pltpu.make_async_copy(
                    OUTB.at[slot, m, :, pl.ds(s * SLAB, SLAB)],
                    w.at[l, :, pl.ds(pl.multiple_of(s * 1024 + f * SLAB, SLAB), SLAB)], s_out.at[slot])
        yield pltpu.make_async_copy(OUTB.at[slot, 2], dwd_out.at[l, tile(f, SLAB), :], s_out.at[slot])

    def wait_outs(slot):
        pltpu.make_async_copy(OUTB.at[slot], RXH.at[0], s_out.at[slot]).wait()

    barrier = pltpu.get_barrier_semaphore()
    for dev in (partner, xnbr, ynbr):
        pl.semaphore_signal(barrier, inc=1, device_id=dev, device_id_type=MESH)

    @pl.loop(0, UNITS)
    def _(u):
        for c in own_loads(u):
            c.start()

    load_x = pltpu.make_async_copy(x_in.at[0], X, s_act.at[0])
    load_dy = pltpu.make_async_copy(dy_in.at[0], DY, s_act.at[1])
    load_x.start()
    load_dy.start()
    pl.semaphore_wait(barrier, 3)

    @pl.loop(0, UNITS // 2)
    def _(k):
        for q in (r, 1 - r):
            u = 2 * k + q
            pltpu.make_async_copy(RXH.at[0], OWN.at[u], s_own.at[u]).wait()
            own_partner(u).start()
            own_home(u).start()
        own_x(k).start()

    load_x.wait()
    load_dy.wait()

    @pl.loop(0, TT // TN)
    def _(t):
        tt = tile(t, TN)
        wide = X[tt, :].astype(f32)
        A[tt, :] = (wide * rms(wide)).astype(bf16)
        DYT[:, tt] = DY[tt, :].T
        ACC[tt, :] = jnp.zeros((TN, D), f32)

    @pl.loop(0, UNITS)
    def _(u):
        own_home(u).wait()

    @pl.loop(0, NF // 2 + 1)
    def _(k):
        arrived_x(k)

        @pl.when(k >= 1)
        def _():
            arrived_y(k - 1)

        @pl.when(k < NF // 2)
        def _():
            fetch_w(2 * k + r, 0)

        @pl.when(k >= 1)
        def _():
            fetch_w(2 * (k - 1) + 1 - r, 1)

        first, last = jnp.where(k < NF // 2, 0, 1), jnp.where(k >= 1, 2, 1)

        @pl.loop(first, last)
        def _(slot):
            load_w(0, slot).wait()

            @pl.loop(0, NT)
            def _(t):
                tt = tile(t, T)
                a = A[tt, :]
                g = dot(a, W[slot, 0])
                up = dot(a, W[slot, 1])
                p = (g * sigmoid(g) * up).astype(bf16)
                ACC[tt, :] += dot(p, W[slot, 2])

    fetch_w(order(0), 0)

    @pl.loop(0, TT // TN)
    def _(t):
        tt = tile(t, TN)
        h = (X[tt, :].astype(f32) + ACC[tt, :].astype(bf16).astype(f32)).astype(bf16)
        H1[tt, :] = h
        wide = h.astype(f32)
        a = (wide * rms(wide)).astype(bf16)
        A[tt, :] = a
        AT[:, tt] = a.T
        ACC[tt, :] = jnp.zeros((TN, D), f32)

    def sum_terms(j):
        slot = j % 2

        @pl.when(j >= 2)
        def _():
            send_sum(0, slot).wait_send()

        for m in range(3):
            OACC[j % 4, m] = KEEP[0, m] + RDV[0, m].astype(f32)
            SX[slot, m] = (KEEP[1, m] + RDV[1, m].astype(f32)).astype(bf16)
        send_sum(order(j), slot).start()

    def finish(j):
        slot = j % 2

        @pl.when(j >= 2)
        def _():
            wait_outs(slot)

        for m in range(3):
            OUTB[slot, m] = (OACC[j % 4, m] + RXV[m].astype(f32)).astype(bf16)
        for c in store_outs(order(j), slot):
            c.start()

    def ask_terms(j):
        send_terms(order(j), 0).wait_recv()
        load_terms(order(j)).start()

    def ask_sum(j):
        send_sum(order(j), 0).wait_recv()
        load_sum(order(j)).start()

    def backward_unit(j):
        slot = j % 2
        load_w(0, slot).wait()

        @pl.loop(0, NT)
        def _(t):
            tt = tile(t, T)
            a = A[tt, :]
            g = dot(a, W[slot, 0])
            up = dot(a, W[slot, 1])
            dp = dot_nt(DY[tt, :], W[slot, 2]).astype(bf16).astype(f32)
            sig = sigmoid(g)
            s = g * sig
            PB[tt, :] = (s * up).astype(bf16)
            du = (dp * s).astype(bf16)
            dg = (dp * up * (sig + s * (1 - sig))).astype(bf16)
            UB[tt, :] = du
            GB[tt, :] = dg
            ACC[tt, :] += dot_nt(dg, W[slot, 0]) + dot_nt(du, W[slot, 1])

            @pl.when((t == 0) & (j >= 1))
            def _():
                ask_terms(j - 1)

            @pl.when((t == 0) & (j >= 3))
            def _():
                ask_sum(j - 3)

        @pl.when(j >= 1)
        def _():
            load_terms(0).wait()
            sum_terms(j - 1)

        @pl.when(j >= 3)
        def _():
            load_sum(0).wait()
            finish(j - 3)

        @pl.when(j >= 2)
        def _():
            send_terms(0, slot).wait_send()

        for m in range(3):
            if m == 0:
                term = dot(AT[...], GB[...])
            elif m == 1:
                term = dot(AT[...], UB[...])
            else:
                term = dot(DYT[...], PB[...]).T
            DWB[...] = term
            KEEP[0, m] = DWB[rows(me), :]
            KEEP[1, m] = DWB[rows(far), :]
            SD[slot, 0, m] = DWB[rows(partner["dp"]), :].astype(bf16)
            SD[slot, 1, m] = DWB[rows((1 - chip) * 2 + 1 - core), :].astype(bf16)
        send_terms(order(j), slot).start()

    def norm_back(h, t):
        wide = h.astype(f32)
        scale = rms(wide)
        da = ACC[tile(t, TN), :].astype(bf16).astype(f32)
        along = jnp.sum(da * wide, -1, keepdims=True) * (scale * scale * scale) * (1.0 / D)
        back = (da * scale - wide * along).astype(bf16)
        return (DY[tile(t, TN), :].astype(f32) + back.astype(f32)).astype(bf16)

    @pl.loop(0, NF)
    def _(j):
        @pl.when(j < 3)
        def _():
            arrived_x(j + 5)

        @pl.when(j < 4)
        def _():
            arrived_y(j + 4)

        backward_unit(j)

        @pl.when(j < NF - 1)
        def _():
            fetch_w(order(j + 1), (j + 1) % 2)

    load_w(order(NF), 0).start()

    @pl.loop(0, TT // TN)
    def _(t):
        tt = tile(t, TN)
        dh = norm_back(H1[tt, :], t)
        DY[tt, :] = dh
        DYT[:, tt] = dh.T
        wide = X[tt, :].astype(f32)
        a = (wide * rms(wide)).astype(bf16)
        A[tt, :] = a
        AT[:, tt] = a.T
        ACC[tt, :] = jnp.zeros((TN, D), f32)

    @pl.loop(NF, UNITS)
    def _(j):
        @pl.when(j < UNITS - 1)
        def _():
            load_w(order(j + 1), (j + 1) % 2).start()

        backward_unit(j)

    @pl.loop(0, TT // TN)
    def _(t):
        tt = tile(t, TN)
        H1[tt, :] = norm_back(X[tt, :], t)

    store_x = pltpu.make_async_copy(H1, bx_out.at[0], s_act.at[0])
    store_x.start()

    last = UNITS - 1
    ask_terms(last)
    load_terms(0).wait()
    sum_terms(last)
    for j in (last - 2, last - 1, last):
        ask_sum(j)
        load_sum(0).wait()
        finish(j)

    store_x.wait()
    for slot in range(2):
        wait_outs(slot)
        send_terms(0, slot).wait_send()
        send_sum(0, slot).wait_send()

    @pl.loop(0, UNITS // 2)
    def _(k):
        own_x(k).wait_send()
        forward_y(k).wait_send()

    @pl.loop(0, UNITS)
    def _(u):
        own_partner(u).wait_send()
        forward_partner(u).wait_send()


def solution(mesh):
    def step(x, dy, w_gate, w_up, w_down):
        vmem, dma = pltpu.VMEM, pltpu.SemaphoreType.DMA
        hbm = pl.BlockSpec(memory_space=pl.ANY)
        shape = jax.ShapeDtypeStruct
        outs = pl.pallas_call(
            kernel,
            out_shape=(
                shape(x.shape, bf16), shape(w_gate.shape, bf16), shape(w_up.shape, bf16), shape(w_down.shape, bf16),
                shape((UNITS, 3, D, FB), bf16), shape((UNITS, 2, 3, SLAB, FB), bf16), shape((UNITS, 3, SLAB, FB), bf16),
            ),
            in_specs=[hbm] * 5,
            out_specs=[hbm] * 7,
            scratch_shapes=[
                vmem((UNITS, 3, SLAB, FB), bf16),
                vmem((2, 3, D, FB), bf16),
                vmem((TT, D), bf16),
                vmem((TT, D), bf16),
                vmem((D, TT), bf16),
                vmem((TT, D), bf16),
                vmem((D, TT), bf16),
                vmem((TT, D), bf16),
                vmem((TT, D), f32),
                vmem((TT, FB), bf16),
                vmem((TT, FB), bf16),
                vmem((TT, FB), bf16),
                vmem((D, FB), f32),
                vmem((2, 3, SLAB, FB), f32),
                vmem((4, 3, SLAB, FB), f32),
                vmem((2, 2, 3, SLAB, FB), bf16),
                vmem((2, 3, SLAB, FB), bf16),
                vmem((2, 3, SLAB, FB), bf16),
                vmem((3, SLAB, FB), bf16),
                vmem((2, 3, SLAB, FB), bf16),
                dma((UNITS,)), dma((UNITS,)),
                dma((UNITS,)), dma((UNITS,)),
                dma((UNITS // 2,)), dma((UNITS // 2,)),
                dma((UNITS // 2,)), dma((UNITS // 2,)),
                dma((UNITS,)), dma((UNITS,)),
                dma((2,)),
                dma((2,)), dma((UNITS,)), dma,
                dma((2,)), dma((UNITS,)), dma,
                dma((2,)), dma((2,)),
            ],
            compiler_params=pltpu.CompilerParams(collective_id=0, has_side_effects=True, vmem_limit_bytes=67_000_000),
            name="stack",
        )(x, dy, w_gate, w_up, w_down)
        return outs[:4]

    tokens, weights = P(("rep", "dp"), None, None), P(None, "dp", None)
    grads = P("rep", "dp", None)
    return jax.shard_map(
        step, mesh=mesh, in_specs=(tokens, tokens, weights, weights, weights),
        out_specs=(tokens, grads, grads, grads), check_vma=False)
```

time: 675 us -> 274 us (0.41); the launches traced: 666 us -> 273 us
  matrix products: 295 us -> 0 us
  Pallas kernels: 0 us -> 263 us
  waiting for transfers between devices: 220 us -> 0 us
  other arithmetic: 110 us -> 0 us
  local copies, waits for them, and re-layouts: 25.1 us -> 9.21 us
  between operations: 15 us -> 0.65 us
    dot_general x17 -> x0, matrix products: 295 us -> none  [the longest x6 122 us: layer(): up = jnp.dot(a, w['w_up'], preferred_element_type=jnp.float32)]
    pallas_call x0 -> x1, Pallas kernels: none -> 263 us  [step(): pl.pallas_call(kernel, out_shape=(shape(x.shape, bf16), shape(w_gate.shap...]
    unnamed x18 -> x0, waiting for transfers between devices: 161 us -> none
    unnamed x3 -> x0, other arithmetic: 87.8 us -> none
    squeeze x6 -> x0, waiting for transfers between devices: 58.8 us -> none  [stack(): h = layer(h, {name: w[number] for name, w in weights.items()})]
    broadcast_in_dim x6 -> x0, other arithmetic: 10.3 us -> none  [stack(): h = layer(h, {name: w[number] for name, w in weights.items()})]
    reshape x4 -> x0, other arithmetic: 9.28 us -> none  [the longest x1 4.91 us: step(): by_x.reshape(shape)]
    unnamed x39 -> x10, local copies, waits for them, and re-layouts: 17.2 us -> 9.21 us
  transfers between devices with their start and end apart: 12 -> 0, of which waited for: 7 -> 0; matrix products, arithmetic and copies ran while one was open for 63% -> 0% of each run, Pallas kernels for 0% -> 0%
where the time goes in v1:
time: 274 us; the launch traced here: 273 us
  Pallas kernels  263 us (96%)
  local copies, waits for them, and re-layouts  9.21 us (3%)
    pallas_call x1, Pallas kernels, step(): pl.pallas_call(kernel, out_shape=(shape(x.shape, bf16), shape(w_gate.shap...  263 us
    unnamed x10, local copies, waits for them, and re-layouts  9.21 us

profile of v1, /device:TPU:0, one launch (start us, length us, event | category | flops | bytes accessed | tf_op | source)
XLA Modules:
  0.0 272.9 jit_solution(9460187442768980488)
XLA Ops:
  0.6 263.0 %stack.1 = (bf16[1,2048,512]{2,1,0:T(8,128)(2,1)}, bf16[2,128,4096]{2,1,0:T(8,128)(2,1)}, bf16[2,128,4096]{2,1,0:T(8,128)(2,1)}, bf16[2,1024,512]{2,1,0:T(8,128)...) custom-call(bf16[1,2048,512]{2,1,0:T(8,128)(2,1)} %x_in.1, ...), custom_call_target="tpu_custom_call" | custom-call | tf_op jit(solution)/shard_map/stack/pallas_call | solution.py:387
  263.7 0.0 copy-start.2
  263.7 3.2 %copy.13 = bf16[1,2048,512]{2,1,0:T(8,128)(2,1)} copy(bf16[1,2048,512]{2,1,0:T(8,128)(2,1)} %get-tuple-element.16) | data formatting | bytes 4194304
  266.9 0.0 copy-done.2
  266.9 0.0 copy-start.1
  266.9 1.3 copy.14
  268.2 1.0 copy-done.1
  269.2 0.0 copy-start
  269.2 1.3 copy.15
  270.6 1.0 copy-done
  271.6 1.3 copy.16
Async XLA Ops:
  263.7 3.2 %copy-start.2 = (bf16[2,128,4096]{2,1,0:T(8,128)(2,1)S(1)}, bf16[2,128,4096]{2,1,0:T(8,128)(2,1)}, u32[]{:S(2)}) copy-start(bf16[2,128,4096]{2,1,0:T(8,128)(2,1)} %get-tuple-element.17) | copy-start | bytes 6291460
  266.9 2.3 copy-start.1
  269.2 2.3 copy-start

commit v2 on v1

v2 whole, which is shorter than its diff:
```python
import jax
import jax.numpy as jnp
from jax import lax
from jax.experimental import pallas as pl
from jax.experimental.pallas import tpu as pltpu
from jax.sharding import PartitionSpec as P

f32, bf16 = jnp.float32, jnp.bfloat16
MESH = pl.DeviceIdType.MESH
TT, D, FF, LAYERS = 2048, 512, 4096, 2
FB = 512
NF = FF // FB
UNITS = LAYERS * NF
PIECES = 3 * UNITS // 2
SLAB = 128
T = 1024
NT = TT // T
TN = 256


def dot(a, b):
    return lax.dot_general(a, b, (((1,), (0,)), ((), ())), preferred_element_type=f32)


def dot_nt(a, b):
    return lax.dot_general(a, b, (((1,), (1,)), ((), ())), preferred_element_type=f32)


def sigmoid(g):
    return 0.5 * jnp.tanh(0.5 * g) + 0.5


def tile(i, size):
    return pl.ds(pl.multiple_of(i * size, size), size)


def rms(wide):
    return lax.rsqrt(jnp.mean(wide * wide, -1, keepdims=True) + 1e-6)


def kernel(
    x_in, dy_in, wg_in, wu_in, wd_in,
    bx_out, dwg_out, dwu_out, dwd_out, WH, RDH, RXH,
    OWN, W, X, A, AT, DY, DYT, H1, ACC, PB, GB, UB, DWB, KEEP, OACC, SD, SX, RDV, RXV, OUTB,
    s_own, s_ownh, s_p, r_p, s_x, r_x, s_y, r_y, s_f, r_f, s_w, s_sd, r_rd, s_rdv, s_sx, r_rx, s_rxv, s_out, s_act,
):
    r, me = lax.axis_index("rep"), lax.axis_index("dp")
    chip, core = me // 2, me % 2
    partner = {"rep": r, "dp": chip * 2 + 1 - core}
    xnbr = {"rep": r, "dp": (1 - chip) * 2 + core}
    ynbr = {"rep": 1 - r, "dp": me}
    far = (1 - chip) * 2 + core

    def rows(d):
        return pl.ds(pl.multiple_of(d * SLAB, SLAB), SLAB)

    def remote(src, dst, send, recv, dev):
        return pltpu.make_async_remote_copy(src_ref=src, dst_ref=dst, send_sem=send, recv_sem=recv, device_id=dev, device_id_type=MESH)

    def order(j):
        return (1 - j // NF) * NF + 2 * ((j % NF) // 2) + lax.rem(r + j, 2)

    def own_loads(u):
        l, f = u // NF, u % NF
        for m, w in enumerate((wg_in, wu_in)):
            for s in range(4):
                yield pltpu.make_async_copy(
                    w.at[l, :, pl.ds(pl.multiple_of(s * 1024 + f * SLAB, SLAB), SLAB)],
                    OWN.at[u, m, :, pl.ds(s * SLAB, SLAB)], s_own.at[u])
        yield pltpu.make_async_copy(wd_in.at[l, tile(f, SLAB), :], OWN.at[u, 2], s_own.at[u])

    def own_home(u):
        return pltpu.make_async_copy(OWN.at[u], WH.at[u, :, rows(me), :], s_ownh.at[u])

    def own_partner(u):
        return remote(OWN.at[u], WH.at[u, :, rows(me), :], s_p.at[u], r_p.at[u], partner)

    def own_x(i):
        u, m = 2 * (i // 3) + r, i % 3
        return remote(OWN.at[u, m], WH.at[u, m, rows(me), :], s_x.at[i], r_x.at[i], xnbr)

    def forward_y(i):
        u, m = 2 * (i // 3) + r, i % 3
        here = WH.at[u, m, rows(far), :]
        return remote(here, here, s_y.at[i], r_y.at[i], ynbr)

    def forward_partner(u, m):
        here = WH.at[u, m, rows(far), :]
        return remote(here, here, s_f.at[u], r_f.at[u], partner)

    def forwarded(u):
        here = WH.at[u, :, rows(far), :]
        return remote(here, here, s_f.at[u], r_f.at[u], partner)

    def arrived_x(i):
        own_x(i).wait_recv()
        forward_y(i).start()
        forward_partner(2 * (i // 3) + r, i % 3).start()

    def arrived_y(i):
        forward_y(i).wait_recv()
        forward_partner(2 * (i // 3) + 1 - r, i % 3).start()

    def load_w(u, slot):
        return pltpu.make_async_copy(WH.at[u], W.at[slot], s_w.at[slot])

    def fetch_w(u, slot):
        own_partner(u).wait_recv()
        forwarded(u).wait_recv()
        load_w(u, slot).start()

    def send_terms(u, slot, m):
        return remote(SD.at[slot, m], RDH.at[u, m], s_sd.at[slot], r_rd.at[u, m], partner)

    def sent_terms(slot):
        remote(SD.at[slot], RDH.at[0], s_sd.at[slot], r_rd.at[0, 0], partner).wait_send()

    def load_terms(u, m):
        return pltpu.make_async_copy(RDH.at[u, m], RDV.at[m], s_rdv.at[m])

    def send_sum(u, slot, m):
        return remote(SX.at[slot, m], RXH.at[u, m], s_sx.at[slot], r_rx.at[u, m], xnbr)

    def sent_sum(slot):
        remote(SX.at[slot], RXH.at[0], s_sx.at[slot], r_rx.at[0, 0], xnbr).wait_send()

    def load_sum(u, m):
        return pltpu.make_async_copy(RXH.at[u, m], RXV.at[m], s_rxv.at[m])

    def store_outs(u, slot):
        l, f = u // NF, u % NF
        for m, w in enumerate((dwg_out, dwu_out)):
            for s in range(4):
                yield pltpu.make_async_copy(
                    OUTB.at[slot, m, :, pl.ds(s * SLAB, SLAB)],
                    w.at[l, :, pl.ds(pl.multiple_of(s * 1024 + f * SLAB, SLAB), SLAB)], s_out.at[slot])
        yield pltpu.make_async_copy(OUTB.at[slot, 2], dwd_out.at[l, tile(f, SLAB), :], s_out.at[slot])

    def wait_outs(slot):
        pltpu.make_async_copy(OUTB.at[slot], RXH.at[0], s_out.at[slot]).wait()

    barrier = pltpu.get_barrier_semaphore()
    for dev in (partner, xnbr, ynbr):
        pl.semaphore_signal(barrier, inc=1, device_id=dev, device_id_type=MESH)

    @pl.loop(0, UNITS)
    def _(u):
        for c in own_loads(u):
            c.start()

    load_x = pltpu.make_async_copy(x_in.at[0], X, s_act.at[0])
    load_dy = pltpu.make_async_copy(dy_in.at[0], DY, s_act.at[1])
    load_x.start()
    load_dy.start()
    pl.semaphore_wait(barrier, 3)

    @pl.loop(0, UNITS // 2)
    def _(k):
        for q in (r, 1 - r):
            u = 2 * k + q
            pltpu.make_async_copy(RXH.at[0], OWN.at[u], s_own.at[u]).wait()
            own_partner(u).start()
            own_home(u).start()
        for m in range(3):
            own_x(3 * k + m).start()

    load_x.wait()
    load_dy.wait()

    @pl.loop(0, TT // TN)
    def _(t):
        tt = tile(t, TN)
        wide = X[tt, :].astype(f32)
        A[tt, :] = (wide * rms(wide)).astype(bf16)
        DYT[:, tt] = DY[tt, :].T
        ACC[tt, :] = jnp.zeros((TN, D), f32)

    @pl.loop(0, UNITS)
    def _(u):
        own_home(u).wait()

    def forward_unit(slot):
        load_w(0, slot).wait()

        @pl.loop(0, NT)
        def _(t):
            tt = tile(t, T)
            a = A[tt, :]
            g = dot(a, W[slot, 0])
            up = dot(a, W[slot, 1])
            p = (g * sigmoid(g) * up).astype(bf16)
            ACC[tt, :] += dot(p, W[slot, 2])

    @pl.loop(0, 3 * NF // 2 + 3)
    def _(i):
        k, m = i // 3, i % 3
        arrived_x(i)

        @pl.when(i >= 2)
        def _():
            arrived_y(i - 2)

        @pl.when((i >= 3) & (m != 1))
        def _():
            @pl.when((m == 0) | (i >= 5))
            def _():
                forward_unit(m // 2)

        @pl.when(m == 2)
        def _():
            @pl.when(k < NF // 2)
            def _():
                fetch_w(2 * k + r, 0)

        @pl.when((m == 1) & (i >= 4))
        def _():
            fetch_w(2 * (k - 1) + 1 - r, 1)

    fetch_w(order(0), 0)

    @pl.loop(0, TT // TN)
    def _(t):
        tt = tile(t, TN)
        h = (X[tt, :].astype(f32) + ACC[tt, :].astype(bf16).astype(f32)).astype(bf16)
        H1[tt, :] = h
        wide = h.astype(f32)
        a = (wide * rms(wide)).astype(bf16)
        A[tt, :] = a
        AT[:, tt] = a.T
        ACC[tt, :] = jnp.zeros((TN, D), f32)

    def ask_terms(j, m):
        send_terms(order(j), 0, m).wait_recv()
        load_terms(order(j), m).start()

    def ask_sum(j, m):
        send_sum(order(j), 0, m).wait_recv()
        load_sum(order(j), m).start()

    def sum_terms(j):
        slot = j % 2

        @pl.when(j >= 2)
        def _():
            sent_sum(slot)

        for m in range(3):
            load_terms(0, m).wait()
            SX[slot, m] = (KEEP[m, 1] + RDV[m, 1].astype(f32)).astype(bf16)
            send_sum(order(j), slot, m).start()
        for m in range(3):
            OACC[j % 4, m] = KEEP[m, 0] + RDV[m, 0].astype(f32)

    def finish(j):
        slot = j % 2

        @pl.when(j >= 2)
        def _():
            wait_outs(slot)

        for m in range(3):
            load_sum(0, m).wait()
            OUTB[slot, m] = (OACC[j % 4, m] + RXV[m].astype(f32)).astype(bf16)
        for c in store_outs(order(j), slot):
            c.start()

    def hidden(t, slot):
        tt = tile(t, T)
        a = A[tt, :]
        g = dot(a, W[slot, 0])
        up = dot(a, W[slot, 1])
        dp = dot_nt(DY[tt, :], W[slot, 2]).astype(bf16).astype(f32)
        sig = sigmoid(g)
        s = g * sig
        PB[tt, :] = (s * up).astype(bf16)
        UB[tt, :] = (dp * s).astype(bf16)
        GB[tt, :] = (dp * up * (sig + s * (1 - sig))).astype(bf16)

    def to_input(t, slot):
        tt = tile(t, T)
        ACC[tt, :] += dot_nt(GB[tt, :], W[slot, 0]) + dot_nt(UB[tt, :], W[slot, 1])

    def terms(j):
        slot = j % 2

        @pl.when(j >= 2)
        def _():
            sent_terms(slot)

        for m in range(3):
            if m == 0:
                DWB[m % 2] = dot(AT[...], GB[...])
            elif m == 1:
                DWB[m % 2] = dot(AT[...], UB[...])
            else:
                DWB[m % 2] = dot(DYT[...], PB[...]).T
            SD[slot, m, 0] = DWB[m % 2, rows(partner["dp"]), :].astype(bf16)
            SD[slot, m, 1] = DWB[m % 2, rows((1 - chip) * 2 + 1 - core), :].astype(bf16)
            send_terms(order(j), slot, m).start()
            KEEP[m, 0] = DWB[m % 2, rows(me), :]
            KEEP[m, 1] = DWB[m % 2, rows(far), :]

    def ask(j):
        for m in range(3):
            ask_terms(j, m)

        @pl.when(j >= 3)
        def _():
            for m in range(3):
                ask_sum(j - 3, m)

    def take(j):
        sum_terms(j)

        @pl.when(j >= 3)
        def _():
            finish(j - 3)

    def layer_back(first, before, after):
        load_w(0, first % 3).wait()

        @pl.loop(0, NT)
        def _(t):
            hidden(t, first % 3)

        @pl.loop(first, first + NF - 1)
        def _(j):
            before(j)
            terms(j)
            load_w(0, (j + 1) % 3).wait()

            @pl.loop(0, NT)
            def _(t):
                to_input(t, j % 3)
                hidden(t, (j + 1) % 3)

                @pl.when(t == 0)
                def _():
                    ask(j)

            take(j)
            after(j)

        last = first + NF - 1
        terms(last)

        @pl.loop(0, NT)
        def _(t):
            to_input(t, last % 3)

            @pl.when(t == 0)
            def _():
                ask(last)

        take(last)

    def norm_back(h, t):
        wide = h.astype(f32)
        scale = rms(wide)
        da = ACC[tile(t, TN), :].astype(bf16).astype(f32)
        along = jnp.sum(da * wide, -1, keepdims=True) * (scale * scale * scale) * (1.0 / D)
        back = (da * scale - wide * along).astype(bf16)
        return (DY[tile(t, TN), :].astype(f32) + back.astype(f32)).astype(bf16)

    def weights_on(j):
        for m in range(3):
            @pl.when(j < 3)
            def _():
                arrived_x(15 + 3 * j + m)

            @pl.when((j >= 1) & (j < 4))
            def _():
                arrived_y(12 + 3 * j + m)

    def before_1(j):
        @pl.when(j == 0)
        def _():
            fetch_w(order(1), 1)

        @pl.when(j >= 1)
        def _():
            weights_on(j)

    def after_1(j):
        @pl.when(j < NF - 2)
        def _():
            fetch_w(order(j + 2), (j + 2) % 3)

        @pl.when(j >= NF - 2)
        def _():
            load_w(order(j + 2), (j + 2) % 3).start()

    weights_on(0)
    for i in (13, 14):
        arrived_y(i)
    layer_back(0, before_1, after_1)
    load_w(order(NF + 1), (NF + 1) % 3).start()

    @pl.loop(0, TT // TN)
    def _(t):
        tt = tile(t, TN)
        dh = norm_back(H1[tt, :], t)
        DY[tt, :] = dh
        DYT[:, tt] = dh.T
        wide = X[tt, :].astype(f32)
        a = (wide * rms(wide)).astype(bf16)
        A[tt, :] = a
        AT[:, tt] = a.T
        ACC[tt, :] = jnp.zeros((TN, D), f32)

    def after_0(j):
        @pl.when(j < UNITS - 2)
        def _():
            load_w(order(j + 2), (j + 2) % 3).start()

    layer_back(NF, lambda j: None, after_0)

    @pl.loop(0, TT // TN)
    def _(t):
        tt = tile(t, TN)
        H1[tt, :] = norm_back(X[tt, :], t)

    store_x = pltpu.make_async_copy(H1, bx_out.at[0], s_act.at[0])
    store_x.start()
    for j in range(UNITS - 3, UNITS):
        for m in range(3):
            ask_sum(j, m)
        finish(j)

    store_x.wait()
    for slot in range(2):
        wait_outs(slot)
        sent_terms(slot)
        sent_sum(slot)

    @pl.loop(0, PIECES)
    def _(i):
        own_x(i).wait_send()
        forward_y(i).wait_send()

    @pl.loop(0, UNITS)
    def _(u):
        own_partner(u).wait_send()
        forwarded(u).wait_send()


def solution(mesh):
    def step(x, dy, w_gate, w_up, w_down):
        vmem, dma = pltpu.VMEM, pltpu.SemaphoreType.DMA
        hbm = pl.BlockSpec(memory_space=pl.ANY)
        shape = jax.ShapeDtypeStruct
        outs = pl.pallas_call(
            kernel,
            out_shape=(
                shape(x.shape, bf16), shape(w_gate.shape, bf16), shape(w_up.shape, bf16), shape(w_down.shape, bf16),
                shape((UNITS, 3, D, FB), bf16), shape((UNITS, 3, 2, SLAB, FB), bf16), shape((UNITS, 3, SLAB, FB), bf16),
            ),
            in_specs=[hbm] * 5,
            out_specs=[hbm] * 7,
            scratch_shapes=[
                vmem((UNITS, 3, SLAB, FB), bf16),
                vmem((3, 3, D, FB), bf16),
                vmem((TT, D), bf16),
                vmem((TT, D), bf16),
                vmem((D, TT), bf16),
                vmem((TT, D), bf16),
                vmem((D, TT), bf16),
                vmem((TT, D), bf16),
                vmem((TT, D), f32),
                vmem((TT, FB), bf16),
                vmem((TT, FB), bf16),
                vmem((TT, FB), bf16),
                vmem((2, D, FB), f32),
                vmem((3, 2, SLAB, FB), f32),
                vmem((4, 3, SLAB, FB), f32),
                vmem((2, 3, 2, SLAB, FB), bf16),
                vmem((2, 3, SLAB, FB), bf16),
                vmem((3, 2, SLAB, FB), bf16),
                vmem((3, SLAB, FB), bf16),
                vmem((2, 3, SLAB, FB), bf16),
                dma((UNITS,)), dma((UNITS,)),
                dma((UNITS,)), dma((UNITS,)),
                dma((PIECES,)), dma((PIECES,)),
                dma((PIECES,)), dma((PIECES,)),
                dma((UNITS,)), dma((UNITS,)),
                dma((3,)),
                dma((2,)), dma((UNITS, 3)), dma((3,)),
                dma((2,)), dma((UNITS, 3)), dma((3,)),
                dma((2,)), dma((2,)),
            ],
            compiler_params=pltpu.CompilerParams(collective_id=0, has_side_effects=True, vmem_limit_bytes=67_000_000),
            name="stack",
        )(x, dy, w_gate, w_up, w_down)
        return outs[:4]

    tokens, weights = P(("rep", "dp"), None, None), P(None, "dp", None)
    grads = P("rep", "dp", None)
    return jax.shard_map(
        step, mesh=mesh, in_specs=(tokens, tokens, weights, weights, weights),
        out_specs=(tokens, grads, grads, grads), check_vma=False)
```

time: 274 us -> 272 us (level)
  no operation moved by 1% of the time
where the time goes in v2:
time: 272 us; the launch traced here: 271 us
  Pallas kernels  261 us (96%)
  local copies, waits for them, and re-layouts  9.21 us (3%)
    pallas_call x1, Pallas kernels, step(): pl.pallas_call(kernel, out_shape=(shape(x.shape, bf16), shape(w_gate.shap...  261 us
    unnamed x10, local copies, waits for them, and re-layouts  9.21 us

profile of v2, /device:TPU:0, one launch (start us, length us, event | category | flops | bytes accessed | tf_op | source)
XLA Modules:
  0.0 271.2 jit_solution(3348050582556318007)
XLA Ops:
  0.6 261.4 %stack.1 = (bf16[1,2048,512]{2,1,0:T(8,128)(2,1)}, bf16[2,128,4096]{2,1,0:T(8,128)(2,1)}, bf16[2,128,4096]{2,1,0:T(8,128)(2,1)}, bf16[2,1024,512]{2,1,0:T(8,128)...) custom-call(bf16[1,2048,512]{2,1,0:T(8,128)(2,1)} %x_in.1, ...), custom_call_target="tpu_custom_call" | custom-call | tf_op jit(solution)/shard_map/stack/pallas_call | solution.py:452
  262.0 0.0 copy-start.2
  262.0 3.2 %copy.13 = bf16[1,2048,512]{2,1,0:T(8,128)(2,1)} copy(bf16[1,2048,512]{2,1,0:T(8,128)(2,1)} %get-tuple-element.16) | data formatting | bytes 4194304
  265.2 0.0 copy-done.2
  265.2 0.0 copy-start.1
  265.2 1.3 copy.14
  266.5 1.0 copy-done.1
  267.6 0.0 copy-start
  267.6 1.3 copy.15
  268.9 1.0 copy-done
  269.9 1.3 copy.16
Async XLA Ops:
  262.0 3.2 %copy-start.2 = (bf16[2,128,4096]{2,1,0:T(8,128)(2,1)S(1)}, bf16[2,128,4096]{2,1,0:T(8,128)(2,1)}, u32[]{:S(2)}) copy-start(bf16[2,128,4096]{2,1,0:T(8,128)(2,1)} %get-tuple-element.17) | copy-start | bytes 6291460
  265.2 2.3 copy-start.1
  267.6 2.3 copy-start

commit v3 on v2

--- a/solution.py
+++ b/solution.py
@@ -40,9 +40,9 @@
 
 def kernel(
     x_in, dy_in, wg_in, wu_in, wd_in,
-    bx_out, dwg_out, dwu_out, dwd_out, WH, RDH, RXH,
-    OWN, W, X, A, AT, DY, DYT, H1, ACC, PB, GB, UB, DWB, KEEP, OACC, SD, SX, RDV, RXV, OUTB,
-    s_own, s_ownh, s_p, r_p, s_x, r_x, s_y, r_y, s_f, r_f, s_w, s_sd, r_rd, s_rdv, s_sx, r_rx, s_rxv, s_out, s_act,
+    bx_out, dwg_out, dwu_out, dwd_out, WH, RDH, RXH, GU,
+    OWN, W, X, A, AT, DY, DYT, H1, ACC, PB, GB, UB, DWB, KEEP, OACC, SD, SX, RDV, RXV, OUTB, GUV,
+    s_own, s_ownh, s_p, r_p, s_x, r_x, s_y, r_y, s_f, r_f, s_w, s_sd, r_rd, s_rdv, s_sx, r_rx, s_rxv, s_out, s_act, s_gu,
 ):
     r, me = lax.axis_index("rep"), lax.axis_index("dp")
     chip, core = me // 2, me % 2
@@ -179,7 +179,13 @@
     def _(u):
         own_home(u).wait()
 
-    def forward_unit(slot):
+    def keep_gu(u, t):
+        return pltpu.make_async_copy(GUV.at[t], GU.at[u, t], s_gu.at[t])
+
+    def load_gu(u, t):
+        return pltpu.make_async_copy(GU.at[u, t], GUV.at[t], s_gu.at[t])
+
+    def forward_unit(u, slot, again):
         load_w(0, slot).wait()
 
         @pl.loop(0, NT)
@@ -188,8 +194,16 @@
             a = A[tt, :]
             g = dot(a, W[slot, 0])
             up = dot(a, W[slot, 1])
+
+            @pl.when(again)
+            def _():
+                keep_gu(0, t).wait()
+
+            GUV[t, 0] = g
+            GUV[t, 1] = up
             p = (g * sigmoid(g) * up).astype(bf16)
             ACC[tt, :] += dot(p, W[slot, 2])
+            keep_gu(u, t).start()
 
     @pl.loop(0, 3 * NF // 2 + 3)
     def _(i):
@@ -204,7 +218,7 @@
         def _():
             @pl.when((m == 0) | (i >= 5))
             def _():
-                forward_unit(m // 2)
+                forward_unit(2 * (k - 1) + lax.rem(r + m // 2, 2), m // 2, i > 3)
 
         @pl.when(m == 2)
         def _():
@@ -217,6 +231,9 @@
             fetch_w(2 * (k - 1) + 1 - r, 1)
 
     fetch_w(order(0), 0)
+    for t in range(NT):
+        keep_gu(0, t).wait()
+        load_gu(order(NF), t).start()
 
     @pl.loop(0, TT // TN)
     def _(t):
@@ -264,17 +281,25 @@
         for c in store_outs(order(j), slot):
             c.start()
 
-    def hidden(t, slot):
+    def hidden(j, t, slot, kept):
         tt = tile(t, T)
-        a = A[tt, :]
-        g = dot(a, W[slot, 0])
-        up = dot(a, W[slot, 1])
+        if kept:
+            load_gu(0, t).wait()
+            g, up = GUV[t, 0], GUV[t, 1]
+        else:
+            a = A[tt, :]
+            g = dot(a, W[slot, 0])
+            up = dot(a, W[slot, 1])
         dp = dot_nt(DY[tt, :], W[slot, 2]).astype(bf16).astype(f32)
         sig = sigmoid(g)
         s = g * sig
         PB[tt, :] = (s * up).astype(bf16)
         UB[tt, :] = (dp * s).astype(bf16)
         GB[tt, :] = (dp * up * (sig + s * (1 - sig))).astype(bf16)
+        if kept:
+            @pl.when(j < UNITS - 1)
+            def _():
+                load_gu(order(j + 1), t).start()
 
     def to_input(t, slot):
         tt = tile(t, T)
@@ -316,12 +341,12 @@
         def _():
             finish(j - 3)
 
-    def layer_back(first, before, after):
+    def layer_back(first, kept, before, after):
         load_w(0, first % 3).wait()
 
         @pl.loop(0, NT)
         def _(t):
-            hidden(t, first % 3)
+            hidden(first, t, first % 3, kept)
 
         @pl.loop(first, first + NF - 1)
         def _(j):
@@ -332,7 +357,7 @@
             @pl.loop(0, NT)
             def _(t):
                 to_input(t, j % 3)
-                hidden(t, (j + 1) % 3)
+                hidden(j + 1, t, (j + 1) % 3, kept)
 
                 @pl.when(t == 0)
                 def _():
@@ -393,7 +418,7 @@
     weights_on(0)
     for i in (13, 14):
         arrived_y(i)
-    layer_back(0, before_1, after_1)
+    layer_back(0, False, before_1, after_1)
     load_w(order(NF + 1), (NF + 1) % 3).start()
 
     @pl.loop(0, TT // TN)
@@ -413,7 +438,7 @@
         def _():
             load_w(order(j + 2), (j + 2) % 3).start()
 
-    layer_back(NF, lambda j: None, after_0)
+    layer_back(NF, True, lambda j: None, after_0)
 
     @pl.loop(0, TT // TN)
     def _(t):
@@ -454,9 +479,10 @@
             out_shape=(
                 shape(x.shape, bf16), shape(w_gate.shape, bf16), shape(w_up.shape, bf16), shape(w_down.shape, bf16),
                 shape((UNITS, 3, D, FB), bf16), shape((UNITS, 3, 2, SLAB, FB), bf16), shape((UNITS, 3, SLAB, FB), bf16),
+                shape((NF, NT, 2, T, FB), f32),
             ),
             in_specs=[hbm] * 5,
-            out_specs=[hbm] * 7,
+            out_specs=[hbm] * 8,
             scratch_shapes=[
                 vmem((UNITS, 3, SLAB, FB), bf16),
                 vmem((3, 3, D, FB), bf16),
@@ -478,6 +504,7 @@
                 vmem((3, 2, SLAB, FB), bf16),
                 vmem((3, SLAB, FB), bf16),
                 vmem((2, 3, SLAB, FB), bf16),
+                vmem((NT, 2, T, FB), f32),
                 dma((UNITS,)), dma((UNITS,)),
                 dma((UNITS,)), dma((UNITS,)),
                 dma((PIECES,)), dma((PIECES,)),
@@ -486,7 +513,7 @@
                 dma((3,)),
                 dma((2,)), dma((UNITS, 3)), dma((3,)),
                 dma((2,)), dma((UNITS, 3)), dma((3,)),
-                dma((2,)), dma((2,)),
+                dma((2,)), dma((2,)), dma((NT,)),
             ],
             compiler_params=pltpu.CompilerParams(collective_id=0, has_side_effects=True, vmem_limit_bytes=67_000_000),
             name="stack",

time: 272 us -> 276 us (1.015)
  Pallas kernels: 261 us -> 265 us
    pallas_call x1, Pallas kernels: 261 us -> 265 us  [step(): pl.pallas_call(kernel, out_shape=(shape(x.shape, bf16), shape(w_gate.shap...]
where the time goes in v3:
time: 276 us; the launch traced here: 275 us
  Pallas kernels  265 us (96%)
  local copies, waits for them, and re-layouts  9.21 us (3%)
    pallas_call x1, Pallas kernels, step(): pl.pallas_call(kernel, out_shape=(shape(x.shape, bf16), shape(w_gate.shap...  265 us
    unnamed x10, local copies, waits for them, and re-layouts  9.21 us

profile of v3, /device:TPU:0, one launch (start us, length us, event | category | flops | bytes accessed | tf_op | source)
XLA Modules:
  0.0 275.3 jit_solution(1056519079555186060)
XLA Ops:
  0.6 265.4 %stack.1 = (bf16[1,2048,512]{2,1,0:T(8,128)(2,1)}, bf16[2,128,4096]{2,1,0:T(8,128)(2,1)}, bf16[2,128,4096]{2,1,0:T(8,128)(2,1)}, bf16[2,1024,512]{2,1,0:T(8,128)...) custom-call(bf16[1,2048,512]{2,1,0:T(8,128)(2,1)} %x_in.1, ...), custom_call_target="tpu_custom_call" | custom-call | tf_op jit(solution)/shard_map/stack/pallas_call | solution.py:477
  266.0 0.0 copy-start.2
  266.0 3.2 %copy.13 = bf16[1,2048,512]{2,1,0:T(8,128)(2,1)} copy(bf16[1,2048,512]{2,1,0:T(8,128)(2,1)} %get-tuple-element.16) | data formatting | bytes 4194304
  269.2 0.0 copy-done.2
  269.2 0.0 copy-start.1
  269.2 1.3 copy.14
  270.6 1.0 copy-done.1
  271.6 0.0 copy-start
  271.6 1.3 copy.15
  272.9 1.0 copy-done
  273.9 1.3 copy.16
Async XLA Ops:
  266.0 3.2 %copy-start.2 = (bf16[2,128,4096]{2,1,0:T(8,128)(2,1)S(1)}, bf16[2,128,4096]{2,1,0:T(8,128)(2,1)}, u32[]{:S(2)}) copy-start(bf16[2,128,4096]{2,1,0:T(8,128)(2,1)} %get-tuple-element.17) | copy-start | bytes 6291460
  269.2 2.3 copy-start.1
  271.6 2.3 copy-start

commit v4 on v3

--- a/solution.py
+++ b/solution.py
@@ -16,6 +16,7 @@
 T = 1024
 NT = TT // T
 TN = 256
+LAG = 2
 
 
 def dot(a, b):
@@ -40,9 +41,9 @@
 
 def kernel(
     x_in, dy_in, wg_in, wu_in, wd_in,
-    bx_out, dwg_out, dwu_out, dwd_out, WH, RDH, RXH, GU,
+    bx_out, dwg_out, dwu_out, dwd_out, WH, RDH, RXH, GU, AT0,
     OWN, W, X, A, AT, DY, DYT, H1, ACC, PB, GB, UB, DWB, KEEP, OACC, SD, SX, RDV, RXV, OUTB, GUV,
-    s_own, s_ownh, s_p, r_p, s_x, r_x, s_y, r_y, s_f, r_f, s_w, s_sd, r_rd, s_rdv, s_sx, r_rx, s_rxv, s_out, s_act, s_gu,
+    s_own, s_ownh, s_p, r_p, s_x, r_x, s_y, r_y, s_f, r_f, s_w, s_sd, r_rd, s_rdv, s_sx, r_rx, s_rxv, s_out, s_act, s_gu, s_at,
 ):
     r, me = lax.axis_index("rep"), lax.axis_index("dp")
     chip, core = me // 2, me % 2
@@ -164,20 +165,22 @@
         for m in range(3):
             own_x(3 * k + m).start()
 
-    load_x.wait()
-    load_dy.wait()
-
-    @pl.loop(0, TT // TN)
-    def _(t):
-        tt = tile(t, TN)
-        wide = X[tt, :].astype(f32)
-        A[tt, :] = (wide * rms(wide)).astype(bf16)
-        DYT[:, tt] = DY[tt, :].T
-        ACC[tt, :] = jnp.zeros((TN, D), f32)
-
-    @pl.loop(0, UNITS)
-    def _(u):
-        own_home(u).wait()
+
+    def norms():
+        @pl.loop(0, TT // TN)
+        def _(t):
+            tt = tile(t, TN)
+            wide = X[tt, :].astype(f32)
+            A[tt, :] = (wide * rms(wide)).astype(bf16)
+            ACC[tt, :] = jnp.zeros((TN, D), f32)
+
+    def turn(src, dst):
+        @pl.loop(0, TT // TN)
+        def _(t):
+            tt = tile(t, TN)
+            dst[:, tt] = src[tt, :].T
+
+    park_a = pltpu.make_async_copy(AT, AT0, s_at)
 
     def keep_gu(u, t):
         return pltpu.make_async_copy(GUV.at[t], GU.at[u, t], s_gu.at[t])
@@ -185,52 +188,81 @@
     def load_gu(u, t):
         return pltpu.make_async_copy(GU.at[u, t], GUV.at[t], s_gu.at[t])
 
-    def forward_unit(u, slot, again):
+    def forward_unit(u, slot, again, halfway):
         load_w(0, slot).wait()
 
         @pl.loop(0, NT)
         def _(t):
             tt = tile(t, T)
+
+            @pl.when(again)
+            def _():
+                keep_gu(0, t).wait()
+
             a = A[tt, :]
             g = dot(a, W[slot, 0])
             up = dot(a, W[slot, 1])
-
-            @pl.when(again)
-            def _():
-                keep_gu(0, t).wait()
-
             GUV[t, 0] = g
             GUV[t, 1] = up
             p = (g * sigmoid(g) * up).astype(bf16)
             ACC[tt, :] += dot(p, W[slot, 2])
             keep_gu(u, t).start()
 
-    @pl.loop(0, 3 * NF // 2 + 3)
+            @pl.when(t == 0)
+            def _():
+                halfway()
+
+    @pl.loop(0, 13 + LAG)
     def _(i):
-        k, m = i // 3, i % 3
         arrived_x(i)
 
-        @pl.when(i >= 2)
-        def _():
-            arrived_y(i - 2)
-
-        @pl.when((i >= 3) & (m != 1))
-        def _():
-            @pl.when((m == 0) | (i >= 5))
-            def _():
-                forward_unit(2 * (k - 1) + lax.rem(r + m // 2, 2), m // 2, i > 3)
-
-        @pl.when(m == 2)
-        def _():
-            @pl.when(k < NF // 2)
-            def _():
-                fetch_w(2 * k + r, 0)
-
-        @pl.when((m == 1) & (i >= 4))
-        def _():
-            fetch_w(2 * (k - 1) + 1 - r, 1)
+        @pl.when(i >= LAG)
+        def _():
+            arrived_y(i - LAG)
+
+        @pl.when(i == 0)
+        def _():
+            load_x.wait()
+            norms()
+
+        @pl.when(i == 1)
+        def _():
+            load_dy.wait()
+            turn(DY, DYT)
+
+            @pl.loop(0, UNITS)
+            def _(u):
+                own_home(u).wait()
+
+        @pl.when(i == 4)
+        def _():
+            turn(A, AT)
+            park_a.start()
+
+        b = (lax.rem(i + 3 - LAG % 3, 3) == 0) & (i >= 3 + LAG)
+        a = (i % 3 == 0) & (i >= 3) & (i < 15)
+        second = jnp.where(b, 1, 0)
+        k = (i - 3 - LAG * second) // 3
+
+        def next_first():
+            @pl.when((i % 3 == 2) & (i < 12))
+            def _():
+                fetch_w(2 * (i // 3) + r, 0)
+
+        @pl.when(a | b)
+        def _():
+            forward_unit(2 * k + lax.rem(r + second, 2), second, i > 3, next_first)
+
+        @pl.when(i == 2)
+        def _():
+            next_first()
+
+        @pl.when((lax.rem(i + 4 - LAG % 3, 3) == 0) & (i >= 2 + LAG))
+        def _():
+            fetch_w(2 * ((i - 2 - LAG) // 3) + 1 - r, 1)
 
     fetch_w(order(0), 0)
+    park_a.wait()
     for t in range(NT):
         keep_gu(0, t).wait()
         load_gu(order(NF), t).start()
@@ -254,6 +286,13 @@
         send_sum(order(j), 0, m).wait_recv()
         load_sum(order(j), m).start()
 
+    def sum_piece(j, m):
+        slot = j % 2
+        load_terms(0, m).wait()
+        SX[slot, m] = (KEEP[m, 1] + RDV[m, 1].astype(f32)).astype(bf16)
+        send_sum(order(j), slot, m).start()
+        OACC[j % 4, m] = KEEP[m, 0] + RDV[m, 0].astype(f32)
+
     def sum_terms(j):
         slot = j % 2
 
@@ -262,11 +301,7 @@
             sent_sum(slot)
 
         for m in range(3):
-            load_terms(0, m).wait()
-            SX[slot, m] = (KEEP[m, 1] + RDV[m, 1].astype(f32)).astype(bf16)
-            send_sum(order(j), slot, m).start()
-        for m in range(3):
-            OACC[j % 4, m] = KEEP[m, 0] + RDV[m, 0].astype(f32)
+            sum_piece(j, m)
 
     def finish(j):
         slot = j % 2
@@ -312,18 +347,21 @@
         def _():
             sent_terms(slot)
 
-        for m in range(3):
-            if m == 0:
-                DWB[m % 2] = dot(AT[...], GB[...])
-            elif m == 1:
-                DWB[m % 2] = dot(AT[...], UB[...])
-            else:
-                DWB[m % 2] = dot(DYT[...], PB[...]).T
-            SD[slot, m, 0] = DWB[m % 2, rows(partner["dp"]), :].astype(bf16)
-            SD[slot, m, 1] = DWB[m % 2, rows((1 - chip) * 2 + 1 - core), :].astype(bf16)
-            send_terms(order(j), slot, m).start()
-            KEEP[m, 0] = DWB[m % 2, rows(me), :]
-            KEEP[m, 1] = DWB[m % 2, rows(far), :]
+        def cut(m):
+            for q, d in enumerate((partner["dp"], (1 - chip) * 2 + 1 - core)):
+                SD[slot, m, q] = DWB[m, rows(d), :].astype(bf16)
+            KEEP[m, 0] = DWB[m, rows(me), :]
+            KEEP[m, 1] = DWB[m, rows(far), :]
+
+        DWB[0] = dot(AT[...], GB[...])
+        DWB[1] = dot(AT[...], UB[...])
+        cut(0)
+        send_terms(order(j), slot, 0).start()
+        DWB[2] = dot(DYT[...], PB[...]).T
+        cut(1)
+        send_terms(order(j), slot, 1).start()
+        cut(2)
+        send_terms(order(j), slot, 2).start()
 
     def ask(j):
         for m in range(3):
@@ -368,6 +406,11 @@
 
         last = first + NF - 1
         terms(last)
+        if not kept:
+            pltpu.make_async_copy(AT0, AT, s_at).start()
+        sent_sum(last % 2)
+        ask_terms(last, 0)
+        ask_terms(last, 1)
 
         @pl.loop(0, NT)
         def _(t):
@@ -375,9 +418,14 @@
 
             @pl.when(t == 0)
             def _():
-                ask(last)
-
-        take(last)
+                sum_piece(last, 0)
+                ask_terms(last, 2)
+                sum_piece(last, 1)
+                for m in range(3):
+                    ask_sum(last - 3, m)
+
+        sum_piece(last, 2)
+        finish(last - 3)
 
     def norm_back(h, t):
         wide = h.astype(f32)
@@ -393,7 +441,7 @@
             def _():
                 arrived_x(15 + 3 * j + m)
 
-            @pl.when((j >= 1) & (j < 4))
+            @pl.when(j < 4)
             def _():
                 arrived_y(12 + 3 * j + m)
 
@@ -415,7 +463,8 @@
         def _():
             load_w(order(j + 2), (j + 2) % 3).start()
 
-    weights_on(0)
+    for i in range(13 + LAG, 18):
+        arrived_x(i)
     for i in (13, 14):
         arrived_y(i)
     layer_back(0, False, before_1, after_1)
@@ -427,11 +476,9 @@
         dh = norm_back(H1[tt, :], t)
         DY[tt, :] = dh
         DYT[:, tt] = dh.T
-        wide = X[tt, :].astype(f32)
-        a = (wide * rms(wide)).astype(bf16)
-        A[tt, :] = a
-        AT[:, tt] = a.T
         ACC[tt, :] = jnp.zeros((TN, D), f32)
+
+    pltpu.make_async_copy(AT0, AT, s_at).wait()
 
     def after_0(j):
         @pl.when(j < UNITS - 2)
@@ -447,6 +494,17 @@
 
     store_x = pltpu.make_async_copy(H1, bx_out.at[0], s_act.at[0])
     store_x.start()
+
+    @pl.loop(0, PIECES)
+    def _(i):
+        own_x(i).wait_send()
+        forward_y(i).wait_send()
+
+    @pl.loop(0, UNITS)
+    def _(u):
+        own_partner(u).wait_send()
+        forwarded(u).wait_send()
+
     for j in range(UNITS - 3, UNITS):
         for m in range(3):
             ask_sum(j, m)
@@ -457,16 +515,6 @@
         wait_outs(slot)
         sent_terms(slot)
         sent_sum(slot)
-
-    @pl.loop(0, PIECES)
-    def _(i):
-        own_x(i).wait_send()
-        forward_y(i).wait_send()
-
-    @pl.loop(0, UNITS)
-    def _(u):
-        own_partner(u).wait_send()
-        forwarded(u).wait_send()
 
 
 def solution(mesh):
@@ -480,9 +528,10 @@
                 shape(x.shape, bf16), shape(w_gate.shape, bf16), shape(w_up.shape, bf16), shape(w_down.shape, bf16),
                 shape((UNITS, 3, D, FB), bf16), shape((UNITS, 3, 2, SLAB, FB), bf16), shape((UNITS, 3, SLAB, FB), bf16),
                 shape((NF, NT, 2, T, FB), f32),
+                shape((D, TT), bf16),
             ),
             in_specs=[hbm] * 5,
-            out_specs=[hbm] * 8,
+            out_specs=[hbm] * 9,
             scratch_shapes=[
                 vmem((UNITS, 3, SLAB, FB), bf16),
                 vmem((3, 3, D, FB), bf16),
@@ -496,7 +545,7 @@
                 vmem((TT, FB), bf16),
                 vmem((TT, FB), bf16),
                 vmem((TT, FB), bf16),
-                vmem((2, D, FB), f32),
+                vmem((3, D, FB), f32),
                 vmem((3, 2, SLAB, FB), f32),
                 vmem((4, 3, SLAB, FB), f32),
                 vmem((2, 3, 2, SLAB, FB), bf16),
@@ -513,7 +562,7 @@
                 dma((3,)),
                 dma((2,)), dma((UNITS, 3)), dma((3,)),
                 dma((2,)), dma((UNITS, 3)), dma((3,)),
-                dma((2,)), dma((2,)), dma((NT,)),
+                dma((2,)), dma((2,)), dma((NT,)), dma,
             ],
             compiler_params=pltpu.CompilerParams(collective_id=0, has_side_effects=True, vmem_limit_bytes=67_000_000),
             name="stack",

time: 276 us -> 260 us (0.942)
  Pallas kernels: 265 us -> 250 us
    pallas_call x1, Pallas kernels: 265 us -> 250 us  [step(): pl.pallas_call(kernel, out_shape=(shape(x.shape, bf16), shape(w_gate.shap...]
where the time goes in v4:
time: 260 us
  Pallas kernels  250 us (96%)
  local copies, waits for them, and re-layouts  9.21 us (4%)
    pallas_call x1, Pallas kernels, step(): pl.pallas_call(kernel, out_shape=(shape(x.shape, bf16), shape(w_gate.shap...  250 us
    unnamed x10, local copies, waits for them, and re-layouts  9.21 us

profile of v4, /device:TPU:0, one launch (start us, length us, event | category | flops | bytes accessed | tf_op | source)
XLA Modules:
  0.0 259.6 jit_solution(4380749984538046805)
XLA Ops:
  0.6 249.8 %stack.1 = (bf16[1,2048,512]{2,1,0:T(8,128)(2,1)}, bf16[2,128,4096]{2,1,0:T(8,128)(2,1)}, bf16[2,128,4096]{2,1,0:T(8,128)(2,1)}, bf16[2,1024,512]{2,1,0:T(8,128)...) custom-call(bf16[1,2048,512]{2,1,0:T(8,128)(2,1)} %x_in.1, ...), custom_call_target="tpu_custom_call" | custom-call | tf_op jit(solution)/shard_map/stack/pallas_call | solution.py:525
  250.4 0.0 copy-start.2
  250.4 3.2 %copy.13 = bf16[1,2048,512]{2,1,0:T(8,128)(2,1)} copy(bf16[1,2048,512]{2,1,0:T(8,128)(2,1)} %get-tuple-element.16) | data formatting | bytes 4194304
  253.6 0.0 copy-done.2
  253.6 0.0 copy-start.1
  253.6 1.3 copy.14
  254.9 1.0 copy-done.1
  256.0 0.0 copy-start
  256.0 1.3 copy.15
  257.3 1.0 copy-done
  258.3 1.3 copy.16
Async XLA Ops:
  250.4 3.2 %copy-start.2 = (bf16[2,128,4096]{2,1,0:T(8,128)(2,1)S(1)}, bf16[2,128,4096]{2,1,0:T(8,128)(2,1)}, u32[]{:S(2)}) copy-start(bf16[2,128,4096]{2,1,0:T(8,128)(2,1)} %get-tuple-element.17) | copy-start | bytes 6291460
  253.6 2.3 copy-start.1
  256.0 2.3 copy-start

commit v5 on v4

--- a/solution.py
+++ b/solution.py
@@ -42,7 +42,7 @@
 def kernel(
     x_in, dy_in, wg_in, wu_in, wd_in,
     bx_out, dwg_out, dwu_out, dwd_out, WH, RDH, RXH, GU, AT0,
-    OWN, W, X, A, AT, DY, DYT, H1, ACC, PB, GB, UB, DWB, KEEP, OACC, SD, SX, RDV, RXV, OUTB, GUV,
+    OWN, W, X, A, AT, DY, DYT, H1, ACC, PB, GB, UB, DWB, OACC, SD, SX, RDV, RXV, OUTB, GUV,
     s_own, s_ownh, s_p, r_p, s_x, r_x, s_y, r_y, s_f, r_f, s_w, s_sd, r_rd, s_rdv, s_sx, r_rx, s_rxv, s_out, s_act, s_gu, s_at,
 ):
     r, me = lax.axis_index("rep"), lax.axis_index("dp")
@@ -263,9 +263,6 @@
 
     fetch_w(order(0), 0)
     park_a.wait()
-    for t in range(NT):
-        keep_gu(0, t).wait()
-        load_gu(order(NF), t).start()
 
     @pl.loop(0, TT // TN)
     def _(t):
@@ -278,6 +275,10 @@
         AT[:, tt] = a.T
         ACC[tt, :] = jnp.zeros((TN, D), f32)
 
+    for t in range(NT):
+        keep_gu(0, t).wait()
+        load_gu(order(NF), t).start()
+
     def ask_terms(j, m):
         send_terms(order(j), 0, m).wait_recv()
         load_terms(order(j), m).start()
@@ -289,9 +290,9 @@
     def sum_piece(j, m):
         slot = j % 2
         load_terms(0, m).wait()
-        SX[slot, m] = (KEEP[m, 1] + RDV[m, 1].astype(f32)).astype(bf16)
+        SX[slot, m] = (DWB[m, rows(far), :] + RDV[m, 1].astype(f32)).astype(bf16)
         send_sum(order(j), slot, m).start()
-        OACC[j % 4, m] = KEEP[m, 0] + RDV[m, 0].astype(f32)
+        OACC[j % 4, m] = DWB[m, rows(me), :] + RDV[m, 0].astype(f32)
 
     def sum_terms(j):
         slot = j % 2
@@ -350,8 +351,6 @@
         def cut(m):
             for q, d in enumerate((partner["dp"], (1 - chip) * 2 + 1 - core)):
                 SD[slot, m, q] = DWB[m, rows(d), :].astype(bf16)
-            KEEP[m, 0] = DWB[m, rows(me), :]
-            KEEP[m, 1] = DWB[m, rows(far), :]
 
         DWB[0] = dot(AT[...], GB[...])
         DWB[1] = dot(AT[...], UB[...])
@@ -392,14 +391,26 @@
             terms(j)
             load_w(0, (j + 1) % 3).wait()
 
-            @pl.loop(0, NT)
-            def _(t):
-                to_input(t, j % 3)
-                hidden(j + 1, t, (j + 1) % 3, kept)
-
-                @pl.when(t == 0)
-                def _():
-                    ask(j)
+            if kept:
+                @pl.loop(0, NT)
+                def _(t):
+                    to_input(t, j % 3)
+
+                ask(j)
+
+                @pl.loop(0, NT)
+                def _(t):
+                    hidden(j + 1, t, (j + 1) % 3, kept)
+
+            else:
+                @pl.loop(0, NT)
+                def _(t):
+                    to_input(t, j % 3)
+                    hidden(j + 1, t, (j + 1) % 3, kept)
+
+                    @pl.when(t == 0)
+                    def _():
+                        ask(j)
 
             take(j)
             after(j)
@@ -515,6 +526,31 @@
         wait_outs(slot)
         sent_terms(slot)
         sent_sum(slot)
+
+
+CHUNKS = 4
+
+
+def hand_over(*refs):
+    srcs, dsts, bufs, (s_in, s_out) = refs[:4], refs[4:8], refs[8:12], refs[12:]
+
+    def chunks():
+        for q in range(CHUNKS):
+            for n, src in enumerate(srcs):
+                lead, size = src.shape[0], src.shape[1]
+                if lead == 1:
+                    yield n, q, (slice(None), pl.ds(q * (size // CHUNKS), size // CHUNKS))
+                else:
+                    half = size * lead // CHUNKS
+                    yield n, q, (pl.ds(q * lead // CHUNKS, 1), pl.ds((q % (CHUNKS // lead)) * half, half))
+
+    for n, q, at in chunks():
+        pltpu.make_async_copy(srcs[n].at[at], bufs[n].at[at], s_in.at[n, q]).start()
+    for n, q, at in chunks():
+        pltpu.make_async_copy(srcs[n].at[at], bufs[n].at[at], s_in.at[n, q]).wait()
+        pltpu.make_async_copy(bufs[n].at[at], dsts[n].at[at], s_out.at[n, q]).start()
+    for n, q, at in chunks():
+        pltpu.make_async_copy(bufs[n].at[at], dsts[n].at[at], s_out.at[n, q]).wait()
 
 
 def solution(mesh):
@@ -546,7 +582,6 @@
                 vmem((TT, FB), bf16),
                 vmem((TT, FB), bf16),
                 vmem((3, D, FB), f32),
-                vmem((3, 2, SLAB, FB), f32),
                 vmem((4, 3, SLAB, FB), f32),
                 vmem((2, 3, 2, SLAB, FB), bf16),
                 vmem((2, 3, SLAB, FB), bf16),
@@ -567,7 +602,15 @@
             compiler_params=pltpu.CompilerParams(collective_id=0, has_side_effects=True, vmem_limit_bytes=67_000_000),
             name="stack",
         )(x, dy, w_gate, w_up, w_down)
-        return outs[:4]
+        parts = outs[:4]
+        return pl.pallas_call(
+            hand_over,
+            out_shape=tuple(shape(p.shape, bf16) for p in parts),
+            in_specs=[hbm] * 4,
+            out_specs=(hbm,) * 4,
+            scratch_shapes=[vmem(p.shape, bf16) for p in parts] + [dma((4, CHUNKS)), dma((4, CHUNKS))],
+            name="hand_over",
+        )(*parts)
 
     tokens, weights = P(("rep", "dp"), None, None), P(None, "dp", None)
     grads = P("rep", "dp", None)

time: 260 us -> 255 us (0.981)
  local copies, waits for them, and re-layouts: 9.21 us -> 0 us
  Pallas kernels: 250 us -> 253 us
    unnamed x10 -> x0, local copies, waits for them, and re-layouts: 9.21 us -> none
    pallas_call x0 -> x1, Pallas kernels: none -> 6.57 us  [step(): pl.pallas_call(hand_over, out_shape=tuple((shape(p.shape, bf16) for p in...]
    pallas_call x1, Pallas kernels: 250 us -> 247 us  [step(): pl.pallas_call(kernel, out_shape=(shape(x.shape, bf16), shape(w_gate.shap...]
where the time goes in v5:
time: 255 us; the launch traced here: 254 us
  Pallas kernels  253 us (99%)
    pallas_call x1, Pallas kernels, step(): pl.pallas_call(kernel, out_shape=(shape(x.shape, bf16), shape(w_gate.shap...  247 us
    pallas_call x1, Pallas kernels, step(): pl.pallas_call(hand_over, out_shape=tuple((shape(p.shape, bf16) for p in...  6.57 us

profile of v5, /device:TPU:0, one launch (start us, length us, event | category | flops | bytes accessed | tf_op | source)
XLA Modules:
  0.0 254.2 jit_solution(11233550365686477603)
XLA Ops:
  0.6 246.8 %stack.1 = (bf16[1,2048,512]{2,1,0:T(8,128)(2,1)}, bf16[2,128,4096]{2,1,0:T(8,128)(2,1)}, bf16[2,128,4096]{2,1,0:T(8,128)(2,1)}, bf16[2,1024,512]{2,1,0:T(8,128)...) custom-call(bf16[1,2048,512]{2,1,0:T(8,128)(2,1)} %x_in.1, ...), custom_call_target="tpu_custom_call" | custom-call | tf_op jit(solution)/shard_map/stack/pallas_call | solution.py:561
  247.5 6.6 %hand_over.1 = (bf16[1,2048,512]{2,1,0:T(8,128)(2,1)}, bf16[2,128,4096]{2,1,0:T(8,128)(2,1)}, bf16[2,128,4096]{2,1,0:T(8,128)(2,1)}, bf16[2,1024,512]{2,1,0:T(8,128)(2,1)}) custom-call(bf16[1,2048,512]{2,1,0:T(8,128)(2,1)} %get-tuple-element.8.refs_0_, bf16[2,128,4096]{2,1,0:T(8,128)(2,1)} %get-tuple-element.9.refs_1_, ...), custom_call_target="tpu_custom_call" | custom-call | tf_op jit(solution)/shard_map/hand_over/pallas_call | solution.py:606
